TPU v7x, 128 devices: a whole 4x4x4 slice. The times are simulated.
128 devices in a mesh: attn: 4 (over x), expert: 32 (over z, y, core).
Axes of the slice: x: 4, y: 4, z: 4, core: 2. Of those that a mesh axis runs over, the one named last changes fastest.
Arguments:
- tokens: bfloat16 [4096, 2880], P(('attn', 'expert')), may hold values from -6 to 6
- expert_ids: int32 [4096, 4], P(('attn', 'expert')), may hold values from 0 to 31, all different within a row; in each aligned block of 32 rows (0 to 31, 32 to 63, ...) at most 12 rows name the same one
- gate_probs: float32 [4096, 4], P(('attn', 'expert')), may hold values from 0.05 to 0.6
- shed_blocks: int32 [32], replicated, may hold values from 0 to 4, as said below
- partner: int32 [32], replicated, may hold values from 0 to 31, as said below
- gate_weight: bfloat16 [32, 2880, 2880], P('expert', None, 'attn'), may hold values from -0.109375 to 0.109375
- up_weight: bfloat16 [32, 2880, 2880], P('expert', None, 'attn'), may hold values from -0.109375 to 0.109375
- down_weight: bfloat16 [32, 2880, 2880], P('expert', 'attn'), may hold values from -0.109375 to 0.109375
Outputs:
- moe_out: bfloat16 [4096, 2880], P(('attn', 'expert'))
Inputs may be any that keep to these rules, and one draw needn't show every extreme that they name: `expert_ids`: in the rows of one device, no expert is named by more than 12 rows; the 4 experts of a token differ. `shed_blocks`: some expert has exactly 4. partner pairs the experts: partner[partner[e]] = e and partner[e] != e.
All inputs are finite; a program needn't handle non-finite values.
Results may differ from a plain program's by a relative error of at most 0.0081.
Values may be sent and summed in bfloat16 or wider, within the bound.
No kernel may reach another device: no remote copies, remote signals or barrier semaphores. Data moves between devices by JAX's collectives and lax.ppermute only.
A program may use at most 128 MiB of HBM per device.

v0:
```python
import jax
import jax.numpy as jnp
from jax import lax
from jax.sharding import Mesh
from jax.sharding import PartitionSpec as P

SHED_MOST = 4
ATTN_EXPERT = ("attn", "expert_0", "expert_1", "expert_2")
EXPERT = ("expert_0", "expert_1", "expert_2")


SWISH_SCALE = 1.702


def nothing_yet(array, identity):
    return jnp.broadcast_to(jnp.asarray(identity, array.dtype), array.shape)


def prefix_by_axis(array, axes, combine, identity):
    before = start = nothing_yet(array, identity)
    total = array
    for axis in reversed(axes):
        devices, mine = (lax.axis_size(axis), lax.axis_index(axis))
        pieces = lax.all_gather(total, axis)
        inside, total = (start, start)
        for k in range(devices):
            passed = k < mine
            total = combine(total, pieces[k])
            inside = jnp.where(passed, total, inside)
        before = combine(inside, before)
    return before


def split_up(array, dim, devices):
    dims = array.shape
    parts = array.reshape(*dims[:dim], devices, dims[dim] // devices, *dims[dim + 1 :])
    return jnp.moveaxis(parts, dim, 0)


def sum_at_owner(array, axis, dim):
    parts = split_up(array, dim, lax.axis_size(axis))
    arrived = lax.all_to_all(parts, axis, split_axis=0, concat_axis=0, tiled=True)
    return arrived.astype(jnp.float32).sum(axis=0)


def lookup(table, indices):
    places = jnp.arange(table.shape[0], dtype=jnp.int32)
    return jnp.sum(jnp.where(indices[:, None] == places[None, :], table[None, :], 0), axis=1)


def add_counts(earlier, later):
    return earlier + later


def activate(rows, gate_w, up_w):
    gate_part = jnp.dot(rows, gate_w, preferred_element_type=jnp.float32)
    up_part = jnp.dot(rows, up_w, preferred_element_type=jnp.float32)
    return (gate_part * jax.nn.sigmoid(SWISH_SCALE * gate_part) * (up_part + 1.0)).astype(
        jnp.bfloat16
    )


def on_device(
    tokens, expert_ids, gate_probs, shed_blocks, partner, gate_weight, up_weight, down_weight
):
    tok_rows, model_width = tokens.shape
    top_count = expert_ids.shape[1]
    expert_count = shed_blocks.shape[0]
    group_count = lax.axis_size("attn")
    capacity = tok_rows * top_count * group_count
    block_size = capacity // 8
    most_rows = min(tok_rows, 3 * tok_rows * top_count // expert_count)
    slot_count = 2 * most_rows
    places = jnp.arange(expert_count, dtype=jnp.int32)
    flat_ids = expert_ids.reshape(-1)
    onehot = (flat_ids[:, None] == places[None, :]).astype(jnp.int32)
    counts = jnp.sum(onehot, axis=0)
    local_rank = jnp.sum((jnp.cumsum(onehot, axis=0) - onehot) * onehot, axis=1)
    offsets = prefix_by_axis(counts, ATTN_EXPERT, add_counts, jnp.zeros_like(counts))
    global_rank = local_rank + jnp.sum(onehot * offsets[None, :], axis=1)
    limit = capacity - block_size * lookup(shed_blocks, partner)
    own_limit = lookup(limit, flat_ids)
    own_shed = lookup(shed_blocks, flat_ids)
    native = global_rank < own_limit
    borrowed = jnp.logical_and(
        jnp.logical_not(native), global_rank < own_limit + block_size * own_shed
    )
    usable = jnp.logical_or(native, borrowed)
    target = jnp.where(usable, flat_ids, -1)
    table_rows = capacity + block_size * SHED_MOST
    target_hot = (target[:, None] == places[None, :]).astype(jnp.int32)
    position = jnp.sum((jnp.cumsum(target_hot, axis=0) - target_hot) * target_hot, axis=1)
    buffer_index = jnp.where(usable, target * slot_count + position, expert_count * slot_count)
    token_rows = jnp.repeat(tokens, top_count, axis=0)
    send_rows = (
        jnp.zeros((expert_count * slot_count, model_width), jnp.bfloat16)
        .at[buffer_index]
        .set(token_rows, mode="drop")
    )
    send_slots = (
        jnp.full((expert_count * slot_count,), table_rows, jnp.int32)
        .at[buffer_index]
        .set(global_rank, mode="drop")
    )
    send_rows = send_rows.reshape(expert_count, slot_count, model_width)
    send_slots = send_slots.reshape(expert_count, slot_count)
    got_rows, got_slots = (
        lax.all_to_all(send_rows, EXPERT, split_axis=0, concat_axis=0, tiled=True),
        lax.all_to_all(send_slots, EXPERT, split_axis=0, concat_axis=0, tiled=True),
    )
    local_table = (
        jnp.zeros((table_rows, model_width), jnp.float32)
        .at[got_slots.reshape(-1)]
        .set(got_rows.reshape(-1, model_width).astype(jnp.float32), mode="drop")
    )
    compact = lax.psum(local_table.astype(jnp.bfloat16), "attn")
    gate_own = gate_weight[0]
    up_own = up_weight[0]
    down_own = down_weight[0]
    hidden_own = activate(compact, gate_own, up_own)
    share = sum_at_owner(
        jnp.dot(hidden_own, down_own, preferred_element_type=jnp.float32).astype(jnp.bfloat16),
        "attn",
        0,
    )
    results = lax.all_gather(share.astype(jnp.bfloat16), "attn", axis=0, tiled=True)
    answers = results[jnp.minimum(got_slots, table_rows - 1)]
    returned = lax.all_to_all(answers, EXPERT, split_axis=0, concat_axis=0, tiled=True)
    flat_back = returned.reshape(expert_count * slot_count, model_width)
    picked = flat_back[jnp.minimum(buffer_index, expert_count * slot_count - 1)]
    weights = jnp.where(usable, gate_probs.reshape(-1), 0.0)
    mixed = picked.astype(jnp.float32) * weights[:, None]
    return mixed.reshape(tok_rows, top_count, model_width).sum(axis=1).astype(jnp.bfloat16)


def solution(mesh):
    split = Mesh(
        mesh.devices.reshape(mesh.shape["attn"], 4, 4, 2),
        ("attn", "expert_0", "expert_1", "expert_2"),
    )
    return jax.shard_map(
        on_device,
        mesh=split,
        in_specs=(
            P(ATTN_EXPERT, None),
            P(ATTN_EXPERT, None),
            P(ATTN_EXPERT, None),
            P(),
            P(),
            P(EXPERT, None, "attn"),
            P(EXPERT, None, "attn"),
            P(EXPERT, "attn", None),
        ),
        out_specs=P(ATTN_EXPERT, None),
        check_vma=False,
    )
```

profile of v0, /device:TPU:0, one launch (start us, length us, event | category | flops | bytes accessed | tf_op | source)
XLA Modules:
  0.0 470.4 jit_solution(2602426872722942839)
XLA Ops:
  6.5 0.8 copy.21
  7.3 0.1 eq.20
  7.4 0.1 fusion.16
  7.5 0.1 fusion.15
  7.6 0.1 reshape.233
  7.7 1.2 dynamic-slice
  9.6 0.2 dynamic-update-slice
  9.9 1.8 all-reduce
  11.7 1.2 dynamic-slice.1
  13.6 0.2 fusion.33
  13.7 9.2 %all-reduce.1 = s32[128]{0:T(128)S(1)} all-reduce(s32[128]{0:T(128)S(1)} %fusion.33), channel_id=3, replica_groups=mesh['attn'=4,'expert_0'=4,'expert_1'=4,'expert_2'=2] {'expert_1'}, use_global_device_ids=true, to_apply=%add.1 | all-reduce | flops 128 | bytes 1024
  22.9 0.1 fusion.37
  23.0 11.0 %all-gather.2 = s32[4,1,32]{2,1,0:T(1,128)S(1)} all-gather(s32[1,1,32]{2,1,0:T(1,128)S(1)} %fusion.37), channel_id=1, replica_groups=mesh['attn'=4,'expert_0'=4,'expert_1'=4,'expert_2'=2] {'expert_0'}, dimensions={0}, use_global_device_ids=true | all-gather | bytes 640 | tf_op jit(solution)/shard_map/all_gather | solution.py:24
  34.0 9.7 %all-gather.3 = s32[4,1,32]{2,1,0:T(1,128)S(1)} all-gather(s32[1,1,32]{2,1,0:T(1,128)S(1)} %slice_add_fusion.3), channel_id=1, replica_groups=mesh['attn'=4,'expert_0'=4,'expert_1'=4,'expert_2'=2] {'attn'}, dimensions={0}, use_global_device_ids=true | all-gather | bytes 640 | tf_op jit(solution)/shard_map/all_gather | solution.py:24
  43.7 0.2 reduce_window_sum.17
  43.9 0.8 select_reduce_fusion.5
  44.7 0.1 fusion.24
  44.8 0.9 select_reduce_fusion.1
  45.7 0.1 fusion.14
  45.8 0.2 reduce_window_sum.18
  46.0 0.2 select_reduce_fusion
  46.2 1.0 scatter_custom_fusion
  47.2 0.7 all_to_all.15
  47.9 3.8 all-to-all-start
  51.7 1.1 broadcast_in_dim.80
  52.8 0.4 reshape.269
  53.2 4.6 scatter_custom_fusion.1
  57.7 1.3 all-to-all-done
  59.0 6.2 %all-to-all-start.1 = ((bf16[32,24,2880]{2,1,0:T(8,128)(2,1)}), bf16[32,24,2880]{2,1,0:T(8,128)(2,1)}, u32[]{:S(2)}, u32[]{:S(2)}) async-start(bf16[32,24,2880]{2,1,0:T(8,128)(2,1)} %bitcast.70), calls=%async_computation.1 | async-start | bytes 9043968 | tf_op jit(solution)/shard_map/all_to_all | solution.py:108
  65.2 0.2 all-reduce.4.cloned.1.call-start
  65.5 0.5 broadcast.319
  66.0 0.7 broadcast_minimum_fusion
  66.7 0.1 reshape.234
  66.8 56.1 %all-to-all-done.1 = bf16[32,24,2880]{2,1,0:T(8,128)(2,1)} async-done(((bf16[32,24,2880]{2,1,0:T(8,128)(2,1)}), bf16[32,24,2880]{2,1,0:T(8,128)(2,1)}, u32[]{:S(2)}, u32[]{:S(2)}) %all-to-all-start.1) | async-done | bytes 4423712 | tf_op jit(solution)/shard_map/all_to_all | solution.py:108
  122.9 13.9 %scatter_custom_fusion.2 = f32[768,2880]{1,0:T(8,128)} fusion(s32[768]{0:T(1024)S(1)} %fusion.20, bf16[768,2880]{1,0:T(8,128)(2,1)} %bitcast.25, f32[]{:T(128)} %constant.17.clone.1), kind=kCustom, calls=%fused_computation.5 | custom fusion | flops 2211840 | bytes 13271044 | tf_op jit(solution)/shard_map/scatter | solution.py:114
  136.8 6.2 %convert_element_type.37 = bf16[768,2880]{1,0:T(8,128)(2,1)} convert(f32[768,2880]{1,0:T(8,128)} %scatter_custom_fusion.2) | non-fusion elementwise | flops 2211840 | bytes 13271040 | tf_op jit(solution)/shard_map/convert_element_type | solution.py:116
  143.0 0.0 all-reduce.4.cloned.1.call-update
  143.0 0.3 all-gather.6.cloned.1.call-start
  143.3 92.2 %all-reduce.4.cloned.1.call-done = bf16[768,2880]{1,0:T(8,128)(2,1)} async-done(((bf16[768,2880]{1,0:T(8,128)(2,1)}), bf16[768,2880]{1,0:T(8,128)(2,1)}) %all-reduce.4.cloned.1.call-update) | async-done | bytes 4423696 | tf_op jit(solution)/shard_map/psum | solution.py:116
  235.5 8.6 %fusion.4 = f32[768,720]{0,1:T(8,128)} fusion(bf16[768,2880]{1,0:T(8,128)(2,1)} %all-reduce.4.cloned.1.call-done, bf16[1,2880,720]{1,2,0:T(8,128)(2,1)} %param.14), kind=kOutput, calls=%fused_computation.10 | convolution fusion | flops 3185049600 | bytes 10782720 | tf_op jit(solution)/shard_map/dot_general | solution.py:57
  244.1 15.6 %convolution_convert_fusion = bf16[768,2880]{0,1:T(8,128)(2,1)} fusion(bf16[1,720,2880]{2,1,0:T(8,128)(2,1)} %param.15, f32[768,720]{0,1:T(8,128)} %fusion.4, bf16[768,2880]{1,0:T(8,128)(2,1)} %all-reduce.4.cloned.1.call-done, bf16[1,2880,720]{1,2,0:T(8,128)(2,1)} %param.13), kind=kOutput, calls=%fused_computation.7 | convolution fusion | flops 6376734720 | bytes 19353600 | tf_op jit(solution)/shard_map/dot_general | solution.py:122
  259.7 6.5 %copy.24 = bf16[768,2880]{1,0:T(8,128)(2,1)} copy(bf16[768,2880]{0,1:T(8,128)(2,1)} %convolution_convert_fusion) | data formatting | bytes 8847360 | tf_op jit(solution)/shard_map/convert_element_type | solution.py:122
  266.2 58.4 %all_to_all.24 = bf16[4,192,2880]{2,1,0:T(8,128)(2,1)} all-to-all(bf16[4,192,2880]{2,1,0:T(8,128)(2,1)} %bitcast.71), channel_id=1, replica_groups=mesh['attn'=4,'expert_0'=4,'expert_1'=4,'expert_2'=2] {'attn'}, dimensions={0} | all-to-all | bytes 8847360 | tf_op jit(solution)/shard_map/all_to_all | solution.py:42
  324.6 4.3 reduce_sum.99
  328.9 0.0 all-gather.6.cloned.1.call-update
  328.9 0.1 reshape.243
  329.0 50.4 %all-gather.6.cloned.1.call-done = bf16[768,2880]{1,0:T(8,128)(2,1)} async-done(((bf16[192,2880]{1,0:T(8,128)(2,1)}), bf16[768,2880]{1,0:T(8,128)(2,1)}) %all-gather.6.cloned.1.call-update) | async-done | bytes 4423696 | tf_op jit(solution)/shard_map/all_gather | solution.py:126
  379.4 12.2 %gather_fusion = bf16[768,2880]{1,0:T(8,128)(2,1)} fusion(bf16[768,2880]{1,0:T(8,128)(2,1)} %all-gather.6.cloned.1.call-done, s32[1024]{0:T(1024)S(1)} %pad_clamp_fusion.1), kind=kCustom, calls=%fused_computation | custom fusion | bytes 8850432 | tf_op jit(solution)/shard_map/gather | solution.py:127
  391.6 0.0 copy-start
  391.7 7.5 %all-to-all-start.3 = ((bf16[32,24,2880]{2,1,0:T(8,128)(2,1)}), bf16[32,24,2880]{2,1,0:T(8,128)(2,1)}, u32[]{:S(2)}, u32[]{:S(2)}) async-start(bf16[32,24,2880]{2,1,0:T(8,128)(2,1)} %bitcast.69), calls=%async_computation.3 | async-start | bytes 9043968 | tf_op jit(solution)/shard_map/all_to_all | solution.py:128
  399.2 0.1 add.200
  399.3 0.1 reduce_sum.100
  399.4 0.1 mul.109
  399.5 0.0 copy-done
  399.5 0.1 copy.25
  399.6 57.2 %all-to-all-done.3 = bf16[32,24,2880]{2,1,0:T(8,128)(2,1)} async-done(((bf16[32,24,2880]{2,1,0:T(8,128)(2,1)}), bf16[32,24,2880]{2,1,0:T(8,128)(2,1)}, u32[]{:S(2)}, u32[]{:S(2)}) %all-to-all-start.3) | async-done | bytes 4423712 | tf_op jit(solution)/shard_map/all_to_all | solution.py:128
  456.8 4.7 gather_fusion.1
  461.5 0.4 reshape.240
  461.9 1.7 multiply_reduce_fusion
  (12 shorter events, 0.1 us)
Async XLA Ops:
  47.9 11.1 %all-to-all-start = ((s32[32,1,24]{2,1,0:T(1,128)}), s32[32,1,24]{2,1,0:T(1,128)S(1)}, u32[]{:S(2)}, u32[]{:S(2)}) async-start(s32[32,1,24]{2,1,0:T(1,128)} %bitcast.14), calls=%async_computation | async-start | bytes 32768 | tf_op jit(solution)/shard_map/all_to_all | solution.py:109
  59.0 63.9 %all-to-all-start.1 = ((bf16[32,24,2880]{2,1,0:T(8,128)(2,1)}), bf16[32,24,2880]{2,1,0:T(8,128)(2,1)}, u32[]{:S(2)}, u32[]{:S(2)}) async-start(bf16[32,24,2880]{2,1,0:T(8,128)(2,1)} %bitcast.70), calls=%async_computation.1 | async-start | bytes 9043968 | tf_op jit(solution)/shard_map/all_to_all | solution.py:108
  65.2 170.3 %all-reduce.4.cloned.1.call-start = ((), (), s32[]{:S(2)}) async-start(), calls=%async_computation.4 | async-start | bytes 9043968 | tf_op jit(solution)/shard_map/psum | solution.py:116
  143.0 236.4 %all-gather.6.cloned.1.call-start = ((), (), s32[]{:S(2)}) async-start(), calls=%async_computation.5 | async-start | bytes 5652480 | tf_op jit(solution)/shard_map/all_gather | solution.py:126
  391.6 7.8 %copy-start = (f32[32,4]{0,1:T(4,128)S(1)}, f32[32,4]{0,1:T(4,128)}, u32[]{:S(2)}) copy-start(f32[32,4]{0,1:T(4,128)} %param.10) | copy-start | bytes 1540
  391.7 65.2 %all-to-all-start.3 = ((bf16[32,24,2880]{2,1,0:T(8,128)(2,1)}), bf16[32,24,2880]{2,1,0:T(8,128)(2,1)}, u32[]{:S(2)}, u32[]{:S(2)}) async-start(bf16[32,24,2880]{2,1,0:T(8,128)(2,1)} %bitcast.69), calls=%async_computation.3 | async-start | bytes 9043968 | tf_op jit(solution)/shard_map/all_to_all | solution.py:128
Sparse Core Ops, SparseCore 0:
  143.2 92.3 all-reduce.3
  329.0 50.3 all-gather.5
where the time goes:
time: 471 us; the launch traced here: 470 us
  waiting for transfers between devices  257 us (55%)
  blocking collectives  90.1 us (19%)
  local copies, waits for them, and re-layouts  36.3 us (8%)
  other arithmetic  29.7 us (6%)
  matrix products  24.2 us (5%)
  starting transfers between devices  18.1 us (4%)
  between operations  14.9 us (3%)
    psum x1, waiting for transfers between devices, on_device(): compact = lax.psum(local_table.astype(jnp.bfloat16), 'attn')  92.2 us
    all_to_all x1, blocking collectives, sum_at_owner(): lax.all_to_all(parts, axis, split_axis=0, concat_axis=0, tiled=True)  58.4 us
    all_to_all x1, waiting for transfers between devices, on_device(): lax.all_to_all(answers, EXPERT, split_axis=0, concat_axis=0, tiled=True)  57.2 us
    all_to_all x1, waiting for transfers between devices, on_device(): lax.all_to_all(send_rows, EXPERT, split_axis=0, concat_axis=0, tiled=True)  56.1 us
    all_gather x1, waiting for transfers between devices, on_device(): lax.all_gather(share.astype(jnp.bfloat16), 'attn', axis=0, tiled=True)  50.4 us
    all_gather x2, blocking collectives, prefix_by_axis(): pieces = lax.all_gather(total, axis)  20.7 us
    dot_general x1, matrix products, on_device(): jnp.dot(hidden_own, down_own, preferred_element_type=jnp.float32)  15.6 us
    scatter x1, other arithmetic, on_device(): local_table = jnp.zeros((table_rows, model_width), jnp.float32).at[got_sl...  13.9 us
  transfers between devices with their start and end apart: 5, of which 5 were waited for; matrix products, arithmetic and copies ran while one was open for 2% of the time, Pallas kernels for 0%

commit v1 on v0

v1 whole, which is shorter than its diff:
```python
import jax
import jax.numpy as jnp
from jax import lax
from jax.experimental import pallas as pl
from jax.experimental.pallas import tpu as pltpu
from jax.sharding import Mesh
from jax.sharding import PartitionSpec as P

SHED_MOST = 4
ATTN_EXPERT = ("attn", "expert_0", "expert_1", "expert_2")
EXPERT = ("expert_0", "expert_1", "expert_2")
SWISH_SCALE = 1.702
BF = jnp.bfloat16
F32 = jnp.float32
META = 16


def iota(shape, dim):
    return lax.broadcasted_iota(jnp.int32, shape, dim)


def pick_kernel(tok, groups, rows_out, width, top, x_ref, par_ref, g_ref, rank_ref, prob_ref):
    span = groups * tok
    blocks = x_ref.shape[0] // span
    total = x_ref.shape[0]
    me, bound = par_ref[0], par_ref[1]
    start = width // 128 * 128
    tail = x_ref[:, start:]
    lanes = tail.shape[1]
    choose = (iota((META, lanes), 1) == iota((META, lanes), 0) + (width - start)).astype(BF)
    meta = lax.dot_general(choose, tail, (((1,), (1,)), ((), ())), preferred_element_type=F32)
    hit = meta[0:top] == me.astype(F32)
    prob = meta[top : 2 * top] + meta[2 * top : 3 * top] + meta[3 * top : 4 * top]
    prob = jnp.sum(jnp.where(hit, prob, 0.0), axis=0, keepdims=True)
    named = jnp.sum(jnp.where(hit, 1.0, 0.0), axis=0, keepdims=True)
    named = jnp.concatenate([named[:, b * span : (b + 1) * span] for b in range(blocks)], axis=0)
    prob = jnp.concatenate([prob[:, b * span : (b + 1) * span] for b in range(blocks)], axis=0)
    r, c = iota((span, span), 0), iota((span, span), 1)
    same = (r // tok) == (c // tok)
    inside = jnp.logical_and(same, r < c).astype(BF)
    less = ((r // tok) < (c // tok)).astype(BF)
    m = named.astype(BF)
    dot = lambda a, b: jnp.dot(a, b, preferred_element_type=F32)
    rb, cb = iota((blocks, blocks), 0), iota((blocks, blocks), 1)
    rank = dot(m, inside)
    rank += dot((cb < rb).astype(BF), dot(m, same.astype(BF)).astype(BF))
    rank += dot(jnp.ones((blocks, blocks), BF), dot(m, less).astype(BF))
    keep = jnp.logical_and(named > 0.5, rank < bound.astype(F32))
    slot = jnp.where(keep, rank, -1.0)
    rank_ref[...] = slot.T
    prob_ref[...] = prob.T
    place = iota((rows_out, span), 0).astype(F32)
    per = 8
    for step in range(blocks // per):
        hot = jnp.concatenate(
            [
                jnp.where(slot[b : b + 1] == place, 1.0, 0.0).astype(BF)
                for b in range(step * per, (step + 1) * per)
            ],
            axis=1,
        )
        part = dot(hot, x_ref[step * per * span : (step + 1) * per * span, :width])
        if step == 0:
            acc = part
        else:
            acc += part
    g_ref[...] = acc.astype(BF)


def ffn_kernel(x_ref, wg_ref, wu_ref, wd_ref, o_ref):
    parts, _, width = x_ref.shape
    gate = up = None
    for b in range(parts):
        x = x_ref[b]
        g = jnp.dot(x, wg_ref[b * width : (b + 1) * width, :], preferred_element_type=F32)
        u = jnp.dot(x, wu_ref[b * width : (b + 1) * width, :], preferred_element_type=F32)
        gate, up = (g, u) if b == 0 else (gate + g, up + u)
    hidden = (gate * jax.nn.sigmoid(SWISH_SCALE * gate) * (up + 1.0)).astype(BF)
    for b in range(parts):
        o_ref[b] = jnp.dot(hidden, wd_ref[b], preferred_element_type=F32).astype(BF)


def place_kernel(y_ref, rank_ref, prob_ref, z_ref):
    span, blocks = rank_ref.shape
    rows = y_ref.shape[0]
    place = iota((span, rows), 1).astype(F32)
    lane = iota((span, blocks), 1)

    def step(b, carry):
        mine = lane == b
        slot = jnp.sum(jnp.where(mine, rank_ref[...], 0.0), axis=1, keepdims=True)
        prob = jnp.sum(jnp.where(mine, prob_ref[...], 0.0), axis=1, keepdims=True)
        hot = jnp.where(slot == place, 1.0, 0.0).astype(BF)
        rows_b = jnp.dot(hot, y_ref[...], preferred_element_type=F32) * prob
        z_ref[pl.ds(pl.multiple_of(b * span, span), span), :] = rows_b.astype(BF)
        return carry

    lax.fori_loop(0, blocks, step, 0)


VMEM = pl.BlockSpec(memory_space=pltpu.VMEM)
SMEM = pl.BlockSpec(memory_space=pltpu.SMEM)


def on_device(
    tokens, expert_ids, gate_probs, shed_blocks, partner, gate_weight, up_weight, down_weight
):
    tok, model = tokens.shape
    top = expert_ids.shape[1]
    experts = shed_blocks.shape[0]
    groups = lax.axis_size("attn")
    width = model // groups
    capacity = tok * top * groups
    block = capacity // 8
    slots = capacity + block * SHED_MOST
    span = groups * tok
    total = span * experts
    me = lax.axis_index(EXPERT)
    mine = shed_blocks[me]
    bound = capacity - block * shed_blocks[partner[me]] + block * mine
    par = jnp.stack([me, bound]).astype(jnp.int32)
    high = lax.reduce_precision(gate_probs, 8, 7)
    rest = gate_probs - high
    middle = lax.reduce_precision(rest, 8, 7)
    meta = jnp.concatenate([expert_ids.astype(F32), high, middle, rest - middle], axis=1).astype(BF)
    columns = jnp.stack(
        [
            jnp.concatenate([tokens[:, b * width : (b + 1) * width], meta], axis=1)
            for b in range(groups)
        ]
    )
    mixed = lax.all_to_all(columns, "attn", 0, 0, tiled=True).reshape(span, width + META)
    everyone = lax.all_gather(mixed, EXPERT, tiled=True)

    picked, rank, prob = pl.pallas_call(
        lambda *refs: pick_kernel(tok, groups, slots, width, top, *refs),
        out_shape=(
            jax.ShapeDtypeStruct((slots, width), BF),
            jax.ShapeDtypeStruct((span, experts), F32),
            jax.ShapeDtypeStruct((span, experts), F32),
        ),
        in_specs=[VMEM, SMEM],
        out_specs=(VMEM, VMEM, VMEM),
        cost_estimate=pl.CostEstimate(
            flops=2 * slots * total * width, bytes_accessed=2 * total * width, transcendentals=0
        ),
        name="pick",
    )(everyone, par)

    rows = lax.all_gather(picked, "attn", tiled=True).reshape(groups, slots, width)
    down = down_weight[0].reshape(-1, groups, width).transpose(1, 0, 2)
    units = gate_weight.shape[2]
    tile = 256
    partial = pl.pallas_call(
        ffn_kernel,
        grid=(slots // tile,),
        out_shape=jax.ShapeDtypeStruct((groups, slots, width), BF),
        in_specs=[
            pl.BlockSpec((groups, tile, width), lambda i: (0, i, 0)),
            pl.BlockSpec((model, units), lambda i: (0, 0)),
            pl.BlockSpec((model, units), lambda i: (0, 0)),
            pl.BlockSpec((groups, units, width), lambda i: (0, 0, 0)),
        ],
        out_specs=pl.BlockSpec((groups, tile, width), lambda i: (0, i, 0)),
        cost_estimate=pl.CostEstimate(
            flops=6 * slots * model * units, bytes_accessed=6 * model * units, transcendentals=0
        ),
        name="ffn",
    )(rows, gate_weight[0], up_weight[0], down)
    summed = lax.psum_scatter(
        partial.reshape(groups * slots, width), "attn", scatter_dimension=0, tiled=True
    )
    spread = pl.pallas_call(
        place_kernel,
        out_shape=jax.ShapeDtypeStruct((total, width), BF),
        in_specs=[VMEM, VMEM, VMEM],
        out_specs=VMEM,
        cost_estimate=pl.CostEstimate(
            flops=2 * slots * total * width, bytes_accessed=2 * total * width, transcendentals=0
        ),
        name="place",
    )(summed, rank, prob)
    home = lax.psum_scatter(spread, EXPERT, scatter_dimension=0, tiled=True)
    back = lax.all_to_all(home.reshape(groups, tok, width), "attn", 0, 0, tiled=True)
    return back.transpose(1, 0, 2).reshape(tok, model)


def solution(mesh):
    split = Mesh(
        mesh.devices.reshape(mesh.shape["attn"], 4, 4, 2),
        ("attn", "expert_0", "expert_1", "expert_2"),
    )
    return jax.shard_map(
        on_device,
        mesh=split,
        in_specs=(
            P(ATTN_EXPERT, None),
            P(ATTN_EXPERT, None),
            P(ATTN_EXPERT, None),
            P(),
            P(),
            P(EXPERT, None, "attn"),
            P(EXPERT, None, "attn"),
            P(EXPERT, "attn", None),
        ),
        out_specs=P(ATTN_EXPERT, None),
        check_vma=False,
    )
```

time: 471 us -> 322 us (0.68)
  blocking collectives: 90.1 us -> 21.2 us
  waiting for transfers between devices: 257 us -> 206 us
  Pallas kernels: 0 us -> 43.6 us
  other arithmetic: 29.7 us -> 2.06 us
  matrix products: 24.2 us -> 0 us
  starting transfers between devices: 18.1 us -> 0.13 us
    reduce_scatter x0 -> x2, waiting for transfers between devices: none -> 138 us  [the longest x1 86.3 us: on_device(): home = lax.psum_scatter(spread, EXPERT, scatter_dimension=0, tiled=True)]
    all_to_all x3 -> x0, waiting for transfers between devices: 115 us -> none  [the longest x1 57.2 us: on_device(): lax.all_to_all(answers, EXPERT, split_axis=0, concat_axis=0, tiled=True)]
    psum x1 -> x0, waiting for transfers between devices: 92.2 us -> none  [on_device(): compact = lax.psum(local_table.astype(jnp.bfloat16), 'attn')]
    pallas_call x0 -> x3, Pallas kernels: none -> 43.6 us  [the longest x1 18 us: on_device(): pl.pallas_call(ffn_kernel, grid=(slots // tile,), out_shape=jax.ShapeDtyp...]
    all_to_all x1 -> x2, blocking collectives: 58.4 us -> 21.2 us  [the longest x1 10.6 us: on_device(): lax.all_to_all(columns, 'attn', 0, 0, tiled=True)]
    dot_general x2 -> x0, matrix products: 24.2 us -> none  [the longest x1 15.6 us: on_device(): jnp.dot(hidden_own, down_own, preferred_element_type=jnp.float32)]
    all_gather x2 -> x0, blocking collectives: 20.7 us -> none  [prefix_by_axis(): pieces = lax.all_gather(total, axis)]
    all_to_all x3 -> x0, starting transfers between devices: 17.6 us -> none  [the longest x1 7.51 us: on_device(): lax.all_to_all(answers, EXPERT, split_axis=0, concat_axis=0, tiled=True)]
  transfers between devices with their start and end apart: 5 -> 4, of which waited for: 5 -> 4; matrix products, arithmetic and copies ran while one was open for 2% -> 9% of each run, Pallas kernels for 0% -> 0%
where the time goes in v1:
time: 322 us; the launch traced here: 321 us
  waiting for transfers between devices  206 us (64%)
  Pallas kernels  43.6 us (14%)
  local copies, waits for them, and re-layouts  32.1 us (10%)
  blocking collectives  21.2 us (7%)
  between operations  16.6 us (5%)
    reduce_scatter x1, waiting for transfers between devices, on_device(): home = lax.psum_scatter(spread, EXPERT, scatter_dimension=0, tiled=True)  86.3 us
    reduce_scatter x1, waiting for transfers between devices, on_device(): lax.psum_scatter(partial.reshape(groups * slots, width), 'attn', scatter_...  51.6 us
    all_gather x1, waiting for transfers between devices, on_device(): everyone = lax.all_gather(mixed, EXPERT, tiled=True)  43 us
    all_gather x1, waiting for transfers between devices, on_device(): lax.all_gather(picked, 'attn', tiled=True).reshape(groups, slots, width)  24.7 us
    unnamed x3, local copies, waits for them, and re-layouts  20.1 us
    pallas_call x1, Pallas kernels, on_device(): pl.pallas_call(ffn_kernel, grid=(slots // tile,), out_shape=jax.ShapeDtyp...  18 us
    pallas_call x1, Pallas kernels, on_device(): pl.pallas_call(place_kernel, out_shape=jax.ShapeDtypeStruct((total, width...  16 us
    all_to_all x1, blocking collectives, on_device(): lax.all_to_all(columns, 'attn', 0, 0, tiled=True)  10.6 us
  transfers between devices with their start and end apart: 4, of which 4 were waited for; matrix products, arithmetic and copies ran while one was open for 9% of the time, Pallas kernels for 0%

profile of v1, /device:TPU:0, one launch (start us, length us, event | category | flops | bytes accessed | tf_op | source)
XLA Modules:
  0.0 321.3 jit_solution(1036685757901276387)
XLA Ops:
  6.5 0.0 all-gather.3.cloned.1.call-start
  6.5 0.7 convert_convert_fusion
  7.2 0.7 fusion
  7.9 0.1 copy.31
  8.0 0.1 copy.28
  8.1 0.1 copy.30
  8.2 0.1 copy.29
  8.3 1.0 fusion.1
  9.3 0.1 concatenate.18
  9.4 0.1 concatenate.19
  9.5 0.1 concatenate.21
  9.6 0.1 concatenate.20
  9.8 10.6 %all_to_all.10 = bf16[4,32,736]{2,1,0:T(8,128)(2,1)} all-to-all(bf16[4,32,736]{2,1,0:T(8,128)(2,1)S(1)} %pad_maximum_fusion), channel_id=1, replica_groups=mesh['attn'=4,'expert_0'=4,'expert_1'=4,'expert_2'=2] {'attn'}, dimensions={0} | all-to-all | bytes 376832 | tf_op jit(solution)/shard_map/all_to_all | solution.py:132
  20.4 0.0 all-gather.3.cloned.1.call-update
  20.4 0.0 all-gather.5.cloned.1.call-start
  20.5 1.3 dynamic_slice.9
  23.8 1.4 fusion.2
  26.6 0.7 pad_add_fusion.refs_1_
  27.2 43.0 %all-gather.3.cloned.1.call-done.refs_0_ = bf16[4096,736]{1,0:T(8,128)(2,1)} async-done(((bf16[128,736]{1,0:T(8,128)(2,1)}), bf16[4096,736]{1,0:T(8,128)(2,1)}) %all-gather.3.cloned.1.call-update) | async-done | bytes 6029328 | tf_op jit(solution)/shard_map/all_gather | solution.py:133
  70.2 9.6 %pick.1 = (bf16[768,720]{1,0:T(8,128)(2,1)}, f32[128,32]{1,0:T(8,128)}, f32[128,32]{1,0:T(8,128)}) custom-call(bf16[4096,736]{1,0:T(8,128)(2,1)} %all-gather.3.cloned.1.call-done.refs_0_, s32[2]{0:T(128)} %pad_add_fusion.refs_1_), custom_call_target="tpu_custom_call" | custom-call | flops 4529848320 | bytes 5898240 | tf_op jit(solution)/shard_map/pick/pallas_call | solution.py:135
  79.8 0.0 all-gather.5.cloned.1.call-update
  79.8 0.0 reduce-scatter.3.cloned.1.call-start
  79.9 6.8 %copy.44 = bf16[1,2880,720]{2,1,0:T(8,128)(2,1)} copy(bf16[1,2880,720]{1,2,0:T(8,128)(2,1)} %param.13) | data formatting | bytes 8294400 | tf_op args[5]
  86.6 6.8 %copy.45 = bf16[1,2880,720]{2,1,0:T(8,128)(2,1)} copy(bf16[1,2880,720]{1,2,0:T(8,128)(2,1)} %param.14) | data formatting | bytes 8294400 | tf_op args[6]
  93.4 6.6 %copy.46 = bf16[1,720,2880]{1,2,0:T(8,128)(2,1)} copy(bf16[1,720,2880]{2,1,0:T(8,128)(2,1)} %param.15) | data formatting | bytes 8294400 | tf_op args[7]
  100.0 6.5 %copy.47 = bf16[720,4,720]{2,0,1:T(8,128)(2,1)} copy(bf16[720,4,720]{0,2,1:T(8,128)(2,1)} %bitcast.15) | data formatting | bytes 8294400 | tf_op jit(solution)/shard_map/reshape;squeeze | solution.py:151
  106.5 24.7 %all-gather.5.cloned.1.call-done = bf16[3072,720]{1,0:T(8,128)(2,1)} async-done(((bf16[768,720]{1,0:T(8,128)(2,1)}), bf16[3072,720]{1,0:T(8,128)(2,1)}) %all-gather.5.cloned.1.call-update) | async-done | bytes 4423696 | tf_op jit(solution)/shard_map/all_gather | solution.py:150
  131.2 18.0 %ffn.1 = bf16[4,768,720]{2,1,0:T(8,128)(2,1)} custom-call(bf16[4,768,720]{2,1,0:T(8,128)(2,1)} %bitcast.27, bf16[2880,720]{1,0:T(8,128)(2,1)} %bitcast.17, bf16[2880,720]{1,0:T(8,128)(2,1)} %bitcast.18, bf16[4,720,720]{2,1,0:T(8,128)(2,1)} %bitcast.19), custom_call_target="tpu_custom_call" | custom-call | flops 9555148800 | bytes 12441600 | tf_op jit(solution)/shard_map/ffn/pallas_call | solution.py:154
  149.2 0.0 reduce-scatter.3.cloned.1.call-update
  149.2 0.0 reduce-scatter.5.cloned.1.call-start
  149.3 51.6 %reduce-scatter.3.cloned.1.call-done.y_ref = bf16[768,720]{1,0:T(8,128)(2,1)} async-done(((bf16[3072,720]{1,0:T(8,128)(2,1)}), bf16[768,720]{1,0:T(8,128)(2,1)}) %reduce-scatter.3.cloned.1.call-update) | async-done | bytes 1105936 | tf_op jit(solution)/shard_map/reduce_scatter | solution.py:170
  200.9 16.0 %place.1 = bf16[4096,720]{1,0:T(8,128)(2,1)} custom-call(bf16[768,720]{1,0:T(8,128)(2,1)} %reduce-scatter.3.cloned.1.call-done.y_ref, f32[128,32]{1,0:T(8,128)} %get-tuple-element.9.rank_ref, f32[128,32]{1,0:T(8,128)} %get-tuple-element.10.prob_ref), custom_call_target="tpu_custom_call" | custom-call | flops 4529848320 | bytes 5898240 | tf_op jit(solution)/shard_map/place/pallas_call | solution.py:173
  216.9 0.0 reduce-scatter.5.cloned.1.call-update
  216.9 86.3 %reduce-scatter.5.cloned.1.call-done = bf16[128,720]{1,0:T(8,128)(2,1)} async-done(((bf16[4096,720]{1,0:T(8,128)(2,1)}), bf16[128,720]{1,0:T(8,128)(2,1)}) %reduce-scatter.5.cloned.1.call-update) | async-done | bytes 184336 | tf_op jit(solution)/shard_map/reduce_scatter | solution.py:183
  303.3 10.5 %all_to_all.11 = bf16[4,32,720]{2,1,0:T(8,128)(2,1)S(1)} all-to-all(bf16[4,32,720]{2,1,0:T(8,128)(2,1)} %bitcast.22), channel_id=1, replica_groups=mesh['attn'=4,'expert_0'=4,'expert_1'=4,'expert_2'=2] {'attn'}, dimensions={0} | all-to-all | bytes 368640 | tf_op jit(solution)/shard_map/all_to_all | solution.py:184
  313.8 0.2 copy.48
  314.0 0.9 reshape.27
  (1 shorter events, 0.0 us)
Async XLA Ops:
  6.5 63.7 %all-gather.3.cloned.1.call-start = ((), (), s32[]{:S(2)}) async-start(), calls=%async_computation.4 | async-start | bytes 6488064 | tf_op jit(solution)/shard_map/all_gather | solution.py:133
  20.4 110.8 %all-gather.5.cloned.1.call-start = ((), (), s32[]{:S(2)}) async-start(), calls=%async_computation.5 | async-start | bytes 5898240 | tf_op jit(solution)/shard_map/all_gather | solution.py:150
  79.8 121.0 %reduce-scatter.3.cloned.1.call-start = ((), (), s32[]{:S(2)}) async-start(), calls=%async_computation.6 | async-start | bytes 5898240 | tf_op jit(solution)/shard_map/reduce_scatter | solution.py:170
  149.2 154.0 %reduce-scatter.5.cloned.1.call-start = ((), (), s32[]{:S(2)}) async-start(), calls=%async_computation.7 | async-start | bytes 6488064 | tf_op jit(solution)/shard_map/reduce_scatter | solution.py:183
Sparse Core Ops, SparseCore 0:
  20.5 49.6 all-gather.2
  80.0 51.1 all-gather.4
  149.3 51.4 reduce-scatter.2
  217.1 86.1 reduce-scatter.4

commit v2 on v1

v2 whole, which is shorter than its diff:
```python
import jax
import jax.numpy as jnp
from jax import lax
from jax.experimental import pallas as pl
from jax.experimental.pallas import tpu as pltpu
from jax.sharding import Mesh
from jax.sharding import PartitionSpec as P

SHED_MOST = 4
ATTN_EXPERT = ("attn", "expert_0", "expert_1", "expert_2")
EXPERT = ("expert_0", "expert_1", "expert_2")
SWISH_SCALE = 1.702
BF = jnp.bfloat16
F32 = jnp.float32

def iota(shape, dim):
    return lax.broadcasted_iota(jnp.int32, shape, dim)


def dot(a, b, dims=((1,), (0,))):
    return lax.dot_general(a, b, (dims, ((), ())), preferred_element_type=F32)


def send_kernel(tok, most, width, top, experts, x_ref, s_ref, r_ref):
    span = x_ref.shape[0]
    per = span // tok * most
    x = x_ref[...]
    ids = x[:, width : width + top].astype(F32)
    lane = iota((span, experts), 1).astype(F32)
    named = [ids[:, k : k + 1] == lane for k in range(top)]
    hits = jnp.where(named[0], 1.0, 0.0)
    for k in range(1, top):
        hits += jnp.where(named[k], 1.0, 0.0)
    r, c = iota((span, span), 0), iota((span, span), 1)
    before = jnp.logical_and(r // tok == c // tok, c < r).astype(BF)
    order = dot(before, hits.astype(BF))
    group = (iota((span, 1), 0) // tok * most).astype(F32)
    place = iota((span, experts * per), 1).astype(F32)
    hot = None
    for k in range(top):
        seat = jnp.sum(jnp.where(named[k], order, 0.0), axis=1, keepdims=True)
        seat = seat + ids[:, k : k + 1] * per + group
        r_ref[:, k : k + 1] = seat
        here = jnp.where(seat == place, 1.0, 0.0)
        hot = here if k == 0 else hot + here
    s_ref[...] = dot(hot.astype(BF), x, ((0,), (0,))).astype(BF)


def pick_kernel(most, width, flag, groups, x_ref, par_ref, g_ref, slot_ref):
    came, slots = x_ref.shape[0], g_ref.shape[1]
    per = groups * most
    blocks = came // per
    bound = par_ref[0].astype(F32)
    start = width // 128 * 128
    tail = x_ref[:, start:]
    lanes = tail.shape[1]
    choose = (iota((8, lanes), 1) == flag - start).astype(BF)
    flags = dot(choose, tail, ((1,), (1,)))[0:1]
    row = iota((1, came), 1)
    group, order = row % per // most, (row % most).astype(F32)
    owner = iota((blocks, came), 0) == iota((blocks, came), 1) // per
    split = jnp.where(owner, flags, 0.0).astype(BF)
    member = iota((came, 128), 0) % per // most == iota((came, 128), 1)
    counts = dot(split, member.astype(BF)).astype(BF)
    rb, cb = iota((blocks, blocks), 0), iota((blocks, blocks), 1)
    rl, cl = iota((128, 128), 0), iota((128, 128), 1)
    lower = dot(counts, (rl < cl).astype(BF)).astype(BF)
    offset = dot((cb < rb).astype(BF), counts) + dot(jnp.ones((blocks, blocks), BF), lower)
    spread = jnp.zeros((blocks, came), F32)
    for a in range(groups):
        spread += jnp.where(group == a, offset[:, a : a + 1], 0.0)
    base = jnp.sum(jnp.where(owner, spread, 0.0), axis=0, keepdims=True)
    rank = base + order
    slot = jnp.where(jnp.logical_and(flags > 0.5, rank < bound), rank, -1.0)
    slot_ref[...] = jnp.broadcast_to(slot, (8, came)).T
    hot = jnp.where(slot == iota((slots, came), 0).astype(F32), 1.0, 0.0).astype(BF)
    g_ref[...] = dot(hot, x_ref[:, :width]).astype(BF).T


def ffn_kernel(x_ref, wg_ref, wu_ref, wd_ref, o_ref):
    gate = dot(wg_ref[...], x_ref[...])
    up = dot(wu_ref[...], x_ref[...])
    hidden = (gate * jax.nn.sigmoid(SWISH_SCALE * gate) * (up + 1.0)).astype(BF)
    o_ref[...] = dot(wd_ref[...], hidden).astype(BF)


def place_kernel(y_ref, slot_ref, z_ref):
    slots = y_ref.shape[1]
    came = z_ref.shape[0]
    hot = jnp.where(slot_ref[:, 0:1] == iota((came, slots), 1).astype(F32), 1.0, 0.0)
    z_ref[...] = dot(hot.astype(BF), y_ref[...], ((1,), (1,))).astype(BF)


def mix_kernel(width, top, b_ref, r_ref, x_ref, o_ref):
    span = x_ref.shape[0]
    place = iota((span, b_ref.shape[0]), 1).astype(F32)
    here = [r_ref[:, k : k + 1] == place for k in range(top)]
    total = None
    for part in range(3):
        first = width + (1 + part) * top
        weight = jnp.zeros(place.shape, F32)
        for k in range(top):
            weight += jnp.where(here[k], x_ref[:, first + k : first + k + 1].astype(F32), 0.0)
        piece = dot(weight.astype(BF), b_ref[...])
        total = piece if part == 0 else total + piece
    o_ref[...] = total.astype(BF)


VMEM = pl.BlockSpec(memory_space=pltpu.VMEM)
SMEM = pl.BlockSpec(memory_space=pltpu.SMEM)


def cost(flops, moved):
    return pl.CostEstimate(flops=flops, bytes_accessed=moved, transcendentals=0)


def exchange(blocks):
    return lax.all_to_all(blocks, EXPERT, split_axis=0, concat_axis=0, tiled=True)


def on_device(
    tokens, expert_ids, gate_probs, shed_blocks, partner, gate_weight, up_weight, down_weight
):
    tok, model = tokens.shape
    top = expert_ids.shape[1]
    experts = shed_blocks.shape[0]
    groups = lax.axis_size("attn")
    width = model // groups
    capacity = tok * top * groups
    block = capacity // 8
    slots = capacity + block * SHED_MOST
    span = groups * tok
    most = min(tok, 3 * tok * top // experts)
    me = lax.axis_index(EXPERT)
    bound = capacity - block * shed_blocks[partner[me]] + block * shed_blocks[me]
    par = bound.reshape(1).astype(jnp.int32)
    high = lax.reduce_precision(gate_probs, 8, 7)
    rest = gate_probs - high
    middle = lax.reduce_precision(rest, 8, 7)
    meta = [expert_ids.astype(F32), high, middle, rest - middle, jnp.ones((tok, 1), F32)]
    flag = width + 4 * top
    meta = jnp.concatenate(meta, axis=1).astype(BF)
    columns = jnp.stack(
        [
            jnp.concatenate([tokens[:, b * width : (b + 1) * width], meta], axis=1)
            for b in range(groups)
        ]
    )
    wide = flag + 1
    mixed = lax.all_to_all(columns, "attn", 0, 0, tiled=True).reshape(span, wide)
    per = groups * most
    came = experts * per

    outgoing, seats = pl.pallas_call(
        lambda *refs: send_kernel(tok, most, width, top, experts, *refs),
        out_shape=(
            jax.ShapeDtypeStruct((came, wide), BF),
            jax.ShapeDtypeStruct((span, top), F32),
        ),
        in_specs=[VMEM],
        out_specs=(VMEM, VMEM),
        cost_estimate=cost(2 * span * came * width, 2 * came * width),
        name="send",
    )(mixed)
    arrived = exchange(outgoing.reshape(experts, per, wide)).reshape(came, wide)

    picked, slot = pl.pallas_call(
        lambda *refs: pick_kernel(most, width, flag, groups, *refs),
        out_shape=(
            jax.ShapeDtypeStruct((width, slots), BF),
            jax.ShapeDtypeStruct((came, 8), F32),
        ),
        in_specs=[VMEM, SMEM],
        out_specs=(VMEM, VMEM),
        cost_estimate=cost(2 * slots * came * width, 2 * came * width),
        name="pick",
    )(arrived, par)

    rows = lax.all_gather(picked, "attn", tiled=True)
    units = gate_weight.shape[2]
    tile = 256
    partial = pl.pallas_call(
        ffn_kernel,
        grid=(slots // tile,),
        out_shape=jax.ShapeDtypeStruct((model, slots), BF),
        in_specs=[
            pl.BlockSpec((model, tile), lambda i: (0, i)),
            pl.BlockSpec((units, model), lambda i: (0, 0)),
            pl.BlockSpec((units, model), lambda i: (0, 0)),
            pl.BlockSpec((model, units), lambda i: (0, 0)),
        ],
        out_specs=pl.BlockSpec((model, tile), lambda i: (0, i)),
        cost_estimate=cost(6 * slots * model * units, 6 * model * units),
        name="ffn",
    )(rows, gate_weight[0].T, up_weight[0].T, down_weight[0].T)
    summed = lax.psum_scatter(partial, "attn", scatter_dimension=0, tiled=True)
    answers = pl.pallas_call(
        place_kernel,
        out_shape=jax.ShapeDtypeStruct((came, width), BF),
        in_specs=[VMEM, VMEM],
        out_specs=VMEM,
        cost_estimate=cost(2 * slots * came * width, 2 * came * width),
        name="place",
    )(summed, slot)
    returned = exchange(answers.reshape(experts, per, width)).reshape(came, width)
    home = pl.pallas_call(
        lambda *refs: mix_kernel(width, top, *refs),
        out_shape=jax.ShapeDtypeStruct((span, width), BF),
        in_specs=[VMEM, VMEM, VMEM],
        out_specs=VMEM,
        cost_estimate=cost(6 * span * came * width, 2 * came * width),
        name="mix",
    )(returned, seats, mixed)
    back = lax.all_to_all(home.reshape(groups, tok, width), "attn", 0, 0, tiled=True)
    return back.transpose(1, 0, 2).reshape(tok, model)


def solution(mesh):
    split = Mesh(
        mesh.devices.reshape(mesh.shape["attn"], 4, 4, 2),
        ("attn", "expert_0", "expert_1", "expert_2"),
    )
    return jax.shard_map(
        on_device,
        mesh=split,
        in_specs=(
            P(ATTN_EXPERT, None),
            P(ATTN_EXPERT, None),
            P(ATTN_EXPERT, None),
            P(),
            P(),
            P(EXPERT, None, "attn"),
            P(EXPERT, None, "attn"),
            P(EXPERT, "attn", None),
        ),
        out_specs=P(ATTN_EXPERT, None),
        check_vma=False,
    )
```

time: 322 us -> 252 us (0.78)
  waiting for transfers between devices: 206 us -> 117 us
  blocking collectives: 21.2 us -> 59.4 us
  local copies, waits for them, and re-layouts: 32.1 us -> 12.1 us
  starting transfers between devices: 0.13 us -> 8.42 us
  Pallas kernels: 43.6 us -> 36.2 us
    reduce_scatter x2 -> x1, waiting for transfers between devices: 138 us -> 49.2 us  [on_device(): summed = lax.psum_scatter(partial, 'attn', scatter_dimension=0, tiled=True)]
    all_to_all x1 -> x2, blocking collectives: 10.6 us -> 49.3 us  [the longest x1 38.6 us: exchange(): lax.all_to_all(blocks, EXPERT, split_axis=0, concat_axis=0, tiled=True)]
    all_gather x2 -> x1, waiting for transfers between devices: 67.7 us -> 38.6 us  [on_device(): rows = lax.all_gather(picked, 'attn', tiled=True)]
    all_to_all x0 -> x1, waiting for transfers between devices: none -> 28.9 us  [exchange(): lax.all_to_all(blocks, EXPERT, split_axis=0, concat_axis=0, tiled=True)]
    unnamed x3 -> x7, local copies, waits for them, and re-layouts: 20.1 us -> 8.05 us
    all_to_all x0 -> x1, starting transfers between devices: none -> 8.34 us  [exchange(): lax.all_to_all(blocks, EXPERT, split_axis=0, concat_axis=0, tiled=True)]
    pallas_call x2 -> x4, Pallas kernels: 25.6 us -> 18.8 us  [the longest x1 6.2 us: on_device(): pl.pallas_call(lambda *refs: pick_kernel(most, width, flag, groups, *refs...]
    another operation x5 -> x4, local copies, waits for them, and re-layouts: 6.9 us -> 0.4 us  [the longest x1 6.5 us: on_device(): down = down_weight[0].reshape(-1, groups, width).transpose(1, 0, 2)]
  transfers between devices with their start and end apart: 4 -> 3, of which waited for: 4 -> 3; matrix products, arithmetic and copies ran while one was open for 9% -> 3% of each run, Pallas kernels for 0% -> 0%
where the time goes in v2:
time: 252 us; the launch traced here: 251 us
  waiting for transfers between devices  117 us (46%)
  blocking collectives  59.4 us (24%)
  Pallas kernels  36.2 us (14%)
  between operations  16.5 us (7%)
  local copies, waits for them, and re-layouts  12.1 us (5%)
  starting transfers between devices  8.42 us (3%)
    reduce_scatter x1, waiting for transfers between devices, on_device(): summed = lax.psum_scatter(partial, 'attn', scatter_dimension=0, tiled=True)  49.2 us
    all_gather x1, waiting for transfers between devices, on_device(): rows = lax.all_gather(picked, 'attn', tiled=True)  38.6 us
    all_to_all x1, blocking collectives, exchange(): lax.all_to_all(blocks, EXPERT, split_axis=0, concat_axis=0, tiled=True)  38.6 us
    all_to_all x1, waiting for transfers between devices, exchange(): lax.all_to_all(blocks, EXPERT, split_axis=0, concat_axis=0, tiled=True)  28.9 us
    pallas_call x1, Pallas kernels, on_device(): pl.pallas_call(ffn_kernel, grid=(slots // tile,), out_shape=jax.ShapeDtyp...  17.4 us
    all_to_all x1, blocking collectives, on_device(): lax.all_to_all(columns, 'attn', 0, 0, tiled=True).reshape(span, wide)  10.6 us
    all_to_all x1, blocking collectives, on_device(): lax.all_to_all(home.reshape(groups, tok, width), 'attn', 0, 0, tiled=True)  10.1 us
    all_to_all x1, starting transfers between devices, exchange(): lax.all_to_all(blocks, EXPERT, split_axis=0, concat_axis=0, tiled=True)  8.34 us
  transfers between devices with their start and end apart: 3, of which 3 were waited for; matrix products, arithmetic and copies ran while one was open for 3% of the time, Pallas kernels for 0%

profile of v2, /device:TPU:0, one launch (start us, length us, event | category | flops | bytes accessed | tf_op | source)
XLA Modules:
  0.0 250.8 jit_solution(237908358772394990)
XLA Ops:
  6.5 0.0 copy-start.2
  6.5 0.0 copy-start.1
  6.5 0.7 convert_convert_fusion
  7.3 0.7 fusion
  7.9 0.1 copy.12
  8.0 0.1 copy.9
  8.1 0.1 copy.11
  8.2 0.1 copy.10
  8.3 1.0 fusion.1
  9.4 0.1 concatenate.18
  9.5 0.1 concatenate.19
  9.6 0.1 concatenate.21
  9.7 0.1 concatenate.20
  9.8 10.6 %all_to_all.20 = bf16[4,32,737]{2,1,0:T(8,128)(2,1)} all-to-all(bf16[4,32,737]{2,1,0:T(8,128)(2,1)S(1)} %pad_maximum_fusion), channel_id=1, replica_groups=mesh['attn'=4,'expert_0'=4,'expert_1'=4,'expert_2'=2] {'attn'}, dimensions={0} | all-to-all | bytes 377344 | tf_op jit(solution)/shard_map/all_to_all | solution.py:150
  20.4 3.8 %send.1 = (bf16[1536,737]{1,0:T(8,128)(2,1)}, f32[128,4]{1,0:T(8,128)}) custom-call(bf16[128,737]{1,0:T(8,128)(2,1)} %bitcast.31), custom_call_target="tpu_custom_call" | custom-call | flops 283115520 | bytes 2211840 | tf_op jit(solution)/shard_map/send/pallas_call | solution.py:154
  24.2 8.3 %all-to-all-start.1 = ((bf16[32,48,737]{2,1,0:T(8,128)(2,1)}), bf16[32,48,737]{2,1,0:T(8,128)(2,1)S(1)}, u32[]{:S(2)}, u32[]{:S(2)}) async-start(bf16[32,48,737]{2,1,0:T(8,128)(2,1)} %bitcast.23), calls=%async_computation.1 | async-start | bytes 4718592 | tf_op jit(solution)/shard_map/all_to_all | solution.py:118
  32.6 0.0 all-gather.2.cloned.1.call-start
  32.6 0.0 copy-done.2
  32.6 0.6 dynamic_slice.9
  34.9 0.0 copy-done.1
  34.9 0.7 fusion.2
  36.8 28.9 %all-to-all-done.1 = bf16[32,48,737]{2,1,0:T(8,128)(2,1)S(1)} async-done(((bf16[32,48,737]{2,1,0:T(8,128)(2,1)}), bf16[32,48,737]{2,1,0:T(8,128)(2,1)S(1)}, u32[]{:S(2)}, u32[]{:S(2)}) %all-to-all-start.1) | async-done | bytes 2264096 | tf_op jit(solution)/shard_map/all_to_all | solution.py:118
  65.7 0.0 copy-start
  65.7 1.4 copy-done
  67.1 6.2 %pick.1 = (bf16[720,768]{1,0:T(8,128)(2,1)}, f32[1536,8]{1,0:T(8,128)}) custom-call(bf16[1536,737]{1,0:T(8,128)(2,1)} %bitcast.22, s32[1]{0:T(128)S(6)} %add.23.refs_1_), custom_call_target="tpu_custom_call" | custom-call | flops 1698693120 | bytes 2211840 | tf_op jit(solution)/shard_map/pick/pallas_call | solution.py:167
  73.3 0.0 all-gather.2.cloned.1.call-update
  73.4 0.0 reduce-scatter.2.cloned.1.call-start
  73.4 6.6 %copy.25 = bf16[1,720,2880]{1,2,0:T(8,128)(2,1)} copy(bf16[1,720,2880]{2,1,0:T(8,128)(2,1)} %param.15) | data formatting | bytes 8294400 | tf_op args[7]
  80.0 38.6 %all-gather.2.cloned.1.call-done.x_ref = bf16[2880,768]{1,0:T(8,128)(2,1)} async-done(((bf16[720,768]{1,0:T(8,128)(2,1)}), bf16[2880,768]{1,0:T(8,128)(2,1)}) %all-gather.2.cloned.1.call-update) | async-done | bytes 4423696 | tf_op jit(solution)/shard_map/all_gather | solution.py:179
  118.7 17.4 %ffn.1 = bf16[2880,768]{1,0:T(8,128)(2,1)} custom-call(bf16[2880,768]{1,0:T(8,128)(2,1)} %all-gather.2.cloned.1.call-done.x_ref, bf16[720,2880]{1,0:T(8,128)(2,1)} %bitcast.34, bf16[720,2880]{1,0:T(8,128)(2,1)} %bitcast.35, bf16[2880,720]{1,0:T(8,128)(2,1)} %bitcast.21), custom_call_target="tpu_custom_call" | custom-call | flops 9555148800 | bytes 12441600 | tf_op jit(solution)/shard_map/ffn/pallas_call | solution.py:182
  136.1 0.0 reduce-scatter.2.cloned.1.call-update
  136.1 49.2 %reduce-scatter.2.cloned.1.call-done.y_ref = bf16[720,768]{1,0:T(8,128)(2,1)} async-done(((bf16[2880,768]{1,0:T(8,128)(2,1)}), bf16[720,768]{1,0:T(8,128)(2,1)}) %reduce-scatter.2.cloned.1.call-update) | async-done | bytes 1105936 | tf_op jit(solution)/shard_map/reduce_scatter | solution.py:196
  185.4 4.9 %place.1 = bf16[1536,720]{1,0:T(8,128)(2,1)} custom-call(bf16[720,768]{1,0:T(8,128)(2,1)} %reduce-scatter.2.cloned.1.call-done.y_ref, f32[1536,8]{1,0:T(8,128)} %get-tuple-element.11.slot_ref), custom_call_target="tpu_custom_call" | custom-call | flops 1698693120 | bytes 2211840 | tf_op jit(solution)/shard_map/place/pallas_call | solution.py:197
  190.3 38.6 %all_to_all.21 = bf16[32,48,720]{2,1,0:T(8,128)(2,1)} all-to-all(bf16[32,48,720]{2,1,0:T(8,128)(2,1)} %bitcast.25), channel_id=1, replica_groups=mesh['attn'=4,'expert_0'=4,'expert_1'=4,'expert_2'=2] {'expert_0','exper..., dimensions={0} | all-to-all | bytes 4423680 | tf_op jit(solution)/shard_map/all_to_all | solution.py:118
  228.9 3.9 %mix.1 = bf16[128,720]{1,0:T(8,128)(2,1)} custom-call(bf16[1536,720]{1,0:T(8,128)(2,1)} %bitcast.24, f32[128,4]{1,0:T(8,128)} %get-tuple-element.12.refs_1_, bf16[128,737]{1,0:T(8,128)(2,1)} %bitcast.32), custom_call_target="tpu_custom_call" | custom-call | flops 849346560 | bytes 2211840 | tf_op jit(solution)/shard_map/mix/pallas_call | solution.py:206
  232.8 10.1 %all_to_all.22 = bf16[4,32,720]{2,1,0:T(8,128)(2,1)S(1)} all-to-all(bf16[4,32,720]{2,1,0:T(8,128)(2,1)} %bitcast.33), channel_id=1, replica_groups=mesh['attn'=4,'expert_0'=4,'expert_1'=4,'expert_2'=2] {'attn'}, dimensions={0} | all-to-all | bytes 368640 | tf_op jit(solution)/shard_map/all_to_all | solution.py:214
  242.9 0.2 copy.26
  243.1 0.9 reshape.36
  (2 shorter events, 0.0 us)
Async XLA Ops:
  6.5 26.1 %copy-start.2 = (s32[32]{0:T(128)S(1)}, s32[32]{0:T(128)}, u32[]{:S(2)}) copy-start(s32[32]{0:T(128)} %param.12) | copy-start | bytes 388
  6.5 28.4 %copy-start.1 = (s32[32]{0:T(128)S(1)}, s32[32]{0:T(128)}, u32[]{:S(2)}) copy-start(s32[32]{0:T(128)} %param.11) | copy-start | bytes 388
  24.2 41.5 %all-to-all-start.1 = ((bf16[32,48,737]{2,1,0:T(8,128)(2,1)}), bf16[32,48,737]{2,1,0:T(8,128)(2,1)S(1)}, u32[]{:S(2)}, u32[]{:S(2)}) async-start(bf16[32,48,737]{2,1,0:T(8,128)(2,1)} %bitcast.23), calls=%async_computation.1 | async-start | bytes 4718592 | tf_op jit(solution)/shard_map/all_to_all | solution.py:118
  32.6 86.1 %all-gather.2.cloned.1.call-start = ((), (), s32[]{:S(2)}) async-start(), calls=%async_computation.5 | async-start | bytes 5529600 | tf_op jit(solution)/shard_map/all_gather | solution.py:179
  65.7 1.4 copy-start
  73.4 112.0 %reduce-scatter.2.cloned.1.call-start = ((), (), s32[]{:S(2)}) async-start(), calls=%async_computation.6 | async-start | bytes 5529600 | tf_op jit(solution)/shard_map/reduce_scatter | solution.py:196
Sparse Core Ops, SparseCore 0:
  73.5 45.1 all-gather.1
  136.3 49.0 reduce-scatter.1
